TPU v7x, 32 devices: a whole 2x2x4 slice. The times are simulated.
32 devices in a mesh: row: 8 (over y, x, core), col: 4 (over z).
Axes of the slice: x: 2, y: 2, z: 4, core: 2. Of those that a mesh axis runs over, the one named last changes fastest.
Arguments:
- density_start: float32 [512, 512], P('row', 'col'), may hold values from -0.5 to 1, as said below
- branches: int32 [6], replicated, may hold values from 0 to 1, as said below
Outputs:
- density: float32 [512, 512], P('row', 'col')
- occupations: float32 [6, 2], replicated
Inputs may be any that keep to these rules, and one draw needn't show every extreme that they name: density_start is symmetric with eigenvalues inside 0 to 1. `branches`: each entry is 0 or 1, and exactly 3 entries are 1.
All inputs are finite; a program needn't handle non-finite values.
Results may differ from a plain program's by a relative error of at most 0.0025.
Values may be sent and summed in bfloat16 or wider, within the bound.
A program may use at most 64 MiB of HBM per device.

v0:
```python
import jax
import jax.numpy as jnp
from jax import lax
from jax.sharding import PartitionSpec as P

ITERS = 6


def taken_in(shard, axis, dim, absorb, state):
    everything = jax.tree.map(lambda a: lax.all_gather(a, axis, axis=dim, tiled=True), shard)
    return absorb(state, everything, jnp.int32(0))


def local_trace(matrix_block, diagonal_mask):
    return jnp.sum(matrix_block * diagonal_mask)


def body(density_start, branches):
    rows_here, cols_here = density_start.shape
    row_first = lax.axis_index("row") * rows_here
    col_first = lax.axis_index("col") * cols_here
    row_ids = row_first + lax.broadcasted_iota(jnp.int32, (rows_here, cols_here), 0)
    col_ids = col_first + lax.broadcasted_iota(jnp.int32, (rows_here, cols_here), 1)
    diagonal_mask = (row_ids == col_ids).astype(jnp.float32)
    size_total = cols_here * lax.axis_size("col")
    density = density_start
    records = []
    for iteration in range(ITERS):
        narrow = density.astype(jnp.bfloat16)
        empty = jnp.zeros((rows_here, cols_here), jnp.float32)
        plain_local = local_trace(density, diagonal_mask)
        row_panel = lax.all_gather(narrow, "col", axis=1, tiled=True)

        def add_rows(accumulated, shard_piece, offset):
            panel_part = lax.dynamic_slice_in_dim(row_panel, offset, shard_piece.shape[0], 1)
            return accumulated + jnp.dot(
                panel_part, shard_piece, preferred_element_type=jnp.float32
            )

        square = taken_in(narrow, "row", 0, add_rows, empty)
        square_local = local_trace(square, diagonal_mask)
        branch_now = branches[iteration]
        records.append(jnp.stack([plain_local, square_local]))
        density = jnp.where(branch_now == 1, 2.0 * density - square, square)
    stacked = jnp.stack(records)
    stacked = lax.psum(stacked, ("row", "col"))
    occupations = stacked / size_total
    return (density, occupations)


def solution(mesh):
    in_specs = (P("row", "col"), P())
    out_specs = (P("row", "col"), P())
    return jax.shard_map(body, mesh=mesh, in_specs=in_specs, out_specs=out_specs, check_vma=False)
```

profile of v0, /device:TPU:0, one launch (start us, length us, event | category | flops | bytes accessed | tf_op | source)
XLA Modules:
  0.0 182.0 jit_solution(16147823306401190443)
XLA Ops:
  0.6 0.0 copy-start
  0.7 1.6 fusion.17
  6.1 0.0 copy-done
  6.1 13.7 %all_gather.36 = bf16[64,512]{1,0:T(8,128)(2,1)S(1)} all-gather(bf16[64,128]{1,0:T(8,128)(2,1)S(1)} %convert_element_type.19), channel_id=1, replica_groups=mesh['row'=8,'col'=4] {'col'}, dimensions={1}, use_global_device_ids=true | all-gather | bytes 81920 | tf_op jit(solution)/shard_map/all_gather | solution.py:32
  19.8 9.2 %all_gather.37 = bf16[512,128]{1,0:T(8,128)(2,1)S(1)} all-gather(bf16[64,128]{1,0:T(8,128)(2,1)S(1)} %convert_element_type.19), channel_id=1, replica_groups=mesh['row'=8,'col'=4] {'row'}, dimensions={0}, use_global_device_ids=true | all-gather | bytes 147456 | tf_op jit(solution)/shard_map/all_gather | solution.py:10
  29.0 0.2 fusion.16
  29.2 12.0 %all_gather.38 = bf16[64,512]{1,0:T(8,128)(2,1)S(1)} all-gather(bf16[64,128]{1,0:T(8,128)(2,1)S(1)} %get-tuple-element.24), channel_id=1, replica_groups=mesh['row'=8,'col'=4] {'col'}, dimensions={1}, use_global_device_ids=true | all-gather | bytes 81920 | tf_op jit(solution)/shard_map/all_gather | solution.py:32
  41.2 9.2 %all_gather.39 = bf16[512,128]{1,0:T(8,128)(2,1)S(1)} all-gather(bf16[64,128]{1,0:T(8,128)(2,1)S(1)} %get-tuple-element.24), channel_id=1, replica_groups=mesh['row'=8,'col'=4] {'row'}, dimensions={0}, use_global_device_ids=true | all-gather | bytes 147456 | tf_op jit(solution)/shard_map/all_gather | solution.py:10
  50.4 0.2 fusion.15
  50.5 12.0 %all_gather.40 = bf16[64,512]{1,0:T(8,128)(2,1)S(1)} all-gather(bf16[64,128]{1,0:T(8,128)(2,1)S(1)} %get-tuple-element.22), channel_id=1, replica_groups=mesh['row'=8,'col'=4] {'col'}, dimensions={1}, use_global_device_ids=true | all-gather | bytes 81920 | tf_op jit(solution)/shard_map/all_gather | solution.py:32
  62.5 8.2 %all_gather.41 = bf16[512,128]{1,0:T(8,128)(2,1)S(1)} all-gather(bf16[64,128]{1,0:T(8,128)(2,1)S(1)} %get-tuple-element.22), channel_id=1, replica_groups=mesh['row'=8,'col'=4] {'row'}, dimensions={0}, use_global_device_ids=true | all-gather | bytes 147456 | tf_op jit(solution)/shard_map/all_gather | solution.py:10
  70.7 0.2 fusion.14
  70.9 12.0 %all_gather.42 = bf16[64,512]{1,0:T(8,128)(2,1)S(1)} all-gather(bf16[64,128]{1,0:T(8,128)(2,1)S(1)} %get-tuple-element.20), channel_id=1, replica_groups=mesh['row'=8,'col'=4] {'col'}, dimensions={1}, use_global_device_ids=true | all-gather | bytes 81920 | tf_op jit(solution)/shard_map/all_gather | solution.py:32
  82.9 9.2 %all_gather.43 = bf16[512,128]{1,0:T(8,128)(2,1)S(1)} all-gather(bf16[64,128]{1,0:T(8,128)(2,1)S(1)} %get-tuple-element.20), channel_id=1, replica_groups=mesh['row'=8,'col'=4] {'row'}, dimensions={0}, use_global_device_ids=true | all-gather | bytes 147456 | tf_op jit(solution)/shard_map/all_gather | solution.py:10
  92.1 0.2 fusion.13
  92.2 12.0 %all_gather.44 = bf16[64,512]{1,0:T(8,128)(2,1)S(1)} all-gather(bf16[64,128]{1,0:T(8,128)(2,1)S(1)} %get-tuple-element.18), channel_id=1, replica_groups=mesh['row'=8,'col'=4] {'col'}, dimensions={1}, use_global_device_ids=true | all-gather | bytes 81920 | tf_op jit(solution)/shard_map/all_gather | solution.py:32
  104.2 8.2 %all_gather.45 = bf16[512,128]{1,0:T(8,128)(2,1)S(1)} all-gather(bf16[64,128]{1,0:T(8,128)(2,1)S(1)} %get-tuple-element.18), channel_id=1, replica_groups=mesh['row'=8,'col'=4] {'row'}, dimensions={0}, use_global_device_ids=true | all-gather | bytes 147456 | tf_op jit(solution)/shard_map/all_gather | solution.py:10
  112.4 0.2 fusion.12
  112.6 12.0 %all_gather.46 = bf16[64,512]{1,0:T(8,128)(2,1)S(1)} all-gather(bf16[64,128]{1,0:T(8,128)(2,1)S(1)} %get-tuple-element.16), channel_id=1, replica_groups=mesh['row'=8,'col'=4] {'col'}, dimensions={1}, use_global_device_ids=true | all-gather | bytes 81920 | tf_op jit(solution)/shard_map/all_gather | solution.py:32
  124.6 9.2 %all_gather.47 = bf16[512,128]{1,0:T(8,128)(2,1)S(1)} all-gather(bf16[64,128]{1,0:T(8,128)(2,1)S(1)} %get-tuple-element.16), channel_id=1, replica_groups=mesh['row'=8,'col'=4] {'row'}, dimensions={0}, use_global_device_ids=true | all-gather | bytes 147456 | tf_op jit(solution)/shard_map/all_gather | solution.py:10
  133.8 1.5 fusion.10
  135.2 1.3 maximum_bitcast_fusion.5
  136.5 0.1 copy.10
  136.6 1.3 maximum_bitcast_fusion.4
  138.0 0.1 copy.9
  138.1 1.3 maximum_bitcast_fusion.3
  139.4 0.1 copy.8
  139.4 1.3 maximum_bitcast_fusion.2
  140.8 0.1 copy.7
  140.9 1.3 maximum_bitcast_fusion.1
  142.2 0.1 copy.6
  142.3 1.3 maximum_bitcast_fusion
  143.6 0.1 copy.5
  143.7 0.1 stack.99
  143.8 37.7 %psum.7 = f32[6,2]{0,1:T(2,128)S(1)} all-reduce(f32[6,2]{0,1:T(2,128)S(1)} %stack.99), channel_id=1, replica_groups=mesh['row'=8,'col'=4] {'row','col'}, use_global_device_ids=true, to_apply=%region_12.13 | all-reduce | flops 12 | bytes 96 | tf_op jit(solution)/shard_map/psum | solution.py:46
  181.5 0.6 broadcast_multiply_fusion
  (3 shorter events, 0.0 us)
Async XLA Ops:
  0.6 5.5 %copy-start = (f32[64,128]{1,0:T(8,128)S(1)}, f32[64,128]{1,0:T(8,128)}, u32[]{:S(2)}) copy-start(f32[64,128]{1,0:T(8,128)} %param.2) | copy-start | bytes 98308
where the time goes:
time: 183 us; the launch traced here: 182 us
  blocking collectives  165 us (90%)
  other arithmetic  8.46 us (5%)
  between operations  4.56 us (2%)
  matrix products  2.26 us (1%)
  local copies, waits for them, and re-layouts  2.23 us (1%)
    all_gather x6, blocking collectives, body(): row_panel = lax.all_gather(narrow, 'col', axis=1, tiled=True)  73.7 us
    all_gather x6, blocking collectives, taken_in(): lax.all_gather(a, axis, axis=dim, tiled=True)  53.2 us
    psum x1, blocking collectives, body(): stacked = lax.psum(stacked, ('row', 'col'))  37.7 us
    another operation x6, other arithmetic, body(): stacked = jnp.stack(records)  7.88 us

commit v1 on v0

--- a/solution.py
+++ b/solution.py
@@ -29,7 +29,8 @@
         narrow = density.astype(jnp.bfloat16)
         empty = jnp.zeros((rows_here, cols_here), jnp.float32)
         plain_local = local_trace(density, diagonal_mask)
-        row_panel = lax.all_gather(narrow, "col", axis=1, tiled=True)
+        sent = jnp.stack([narrow] * lax.axis_size("col"))
+        row_panel = jnp.concatenate(lax.all_to_all(sent, "col", 0, 0), axis=1)
 
         def add_rows(accumulated, shard_piece, offset):
             panel_part = lax.dynamic_slice_in_dim(row_panel, offset, shard_piece.shape[0], 1)

time: 183 us -> 147 us (0.80)
  blocking collectives: 165 us -> 93 us
  starting transfers between devices: 0 us -> 31.9 us
  local copies, waits for them, and re-layouts: 2.23 us -> 5.16 us
    all_gather x6 -> x0, blocking collectives: 73.7 us -> none  [body(): row_panel = lax.all_gather(narrow, 'col', axis=1, tiled=True)]
    all_to_all x0 -> x6, starting transfers between devices: none -> 31.9 us  [body(): row_panel = jnp.concatenate(lax.all_to_all(sent, 'col', 0, 0), axis=1)]
    another operation x0 -> x6, local copies, waits for them, and re-layouts: none -> 3.8 us  [body(): sent = jnp.stack([narrow] * lax.axis_size('col'))]
    psum x1, blocking collectives: 37.7 us -> 39.8 us  [body(): stacked = lax.psum(stacked, ('row', 'col'))]
  transfers between devices with their start and end apart: 0 -> 6, of which waited for: 0 -> 0; matrix products, arithmetic and copies ran while one was open for 0% -> 0% of each run, Pallas kernels for 0% -> 0%
where the time goes in v1:
time: 147 us; the launch traced here: 146 us
  blocking collectives  93 us (63%)
  starting transfers between devices  31.9 us (22%)
  other arithmetic  9.29 us (6%)
  local copies, waits for them, and re-layouts  5.16 us (4%)
  between operations  4.46 us (3%)
  matrix products  2.27 us (2%)
    all_gather x6, blocking collectives, taken_in(): lax.all_gather(a, axis, axis=dim, tiled=True)  53.2 us
    psum x1, blocking collectives, body(): stacked = lax.psum(stacked, ('row', 'col'))  39.8 us
    all_to_all x6, starting transfers between devices, body(): row_panel = jnp.concatenate(lax.all_to_all(sent, 'col', 0, 0), axis=1)  31.9 us
    another operation x6, other arithmetic, body(): stacked = jnp.stack(records)  7.96 us
    another operation x6, local copies, waits for them, and re-layouts, body(): sent = jnp.stack([narrow] * lax.axis_size('col'))  3.8 us
  transfers between devices with their start and end apart: 6, of which 0 were waited for; matrix products, arithmetic and copies ran while one was open for 0% of the time, Pallas kernels for 0%

profile of v1, /device:TPU:0, one launch (start us, length us, event | category | flops | bytes accessed | tf_op | source)
XLA Modules:
  0.0 146.1 jit_solution(2799619118825802830)
XLA Ops:
  0.6 0.8 convert_element_type.19
  1.4 0.6 stack.117
  2.0 0.0 copy-start.1
  2.0 6.5 %all-to-all-start = ((bf16[4,64,128]{2,1,0:T(8,128)(2,1)}), bf16[4,64,128]{2,1,0:T(8,128)(2,1)S(1)}, u32[]{:S(2)}, u32[]{:S(2)}) async-start(bf16[4,64,128]{2,1,0:T(8,128)(2,1)} %stack.117), calls=%async_computation | async-start | bytes 131072 | tf_op jit(solution)/shard_map/all_to_all | solution.py:33
  8.5 0.0 copy-done.1
  8.5 0.7 fusion.35
  9.9 0.0 copy-start
  9.9 9.2 %all_gather.18 = bf16[512,128]{1,0:T(8,128)(2,1)S(1)} all-gather(bf16[64,128]{1,0:T(8,128)(2,1)S(1)} %convert_element_type.19), channel_id=1, replica_groups=mesh['row'=8,'col'=4] {'row'}, dimensions={0}, use_global_device_ids=true | all-gather | bytes 147456 | tf_op jit(solution)/shard_map/all_gather | solution.py:10
  19.1 0.0 all-to-all-done
  19.1 0.0 copy-done
  19.1 0.2 fusion.34
  19.3 0.6 stack.118
  19.9 5.1 %all-to-all-start.1 = ((bf16[4,64,128]{2,1,0:T(8,128)(2,1)}), bf16[4,64,128]{2,1,0:T(8,128)(2,1)S(1)}, u32[]{:S(2)}, u32[]{:S(2)}) async-start(bf16[4,64,128]{2,1,0:T(8,128)(2,1)} %stack.118), calls=%async_computation.1 | async-start | bytes 131072 | tf_op jit(solution)/shard_map/all_to_all | solution.py:33
  25.6 9.2 %all_gather.19 = bf16[512,128]{1,0:T(8,128)(2,1)S(1)} all-gather(bf16[64,128]{1,0:T(8,128)(2,1)S(1)} %get-tuple-element.26), channel_id=1, replica_groups=mesh['row'=8,'col'=4] {'row'}, dimensions={0}, use_global_device_ids=true | all-gather | bytes 147456 | tf_op jit(solution)/shard_map/all_gather | solution.py:10
  34.8 0.0 all-to-all-done.1
  34.8 0.2 fusion.33
  34.9 0.6 stack.119
  35.6 5.1 %all-to-all-start.2 = ((bf16[4,64,128]{2,1,0:T(8,128)(2,1)}), bf16[4,64,128]{2,1,0:T(8,128)(2,1)S(1)}, u32[]{:S(2)}, u32[]{:S(2)}) async-start(bf16[4,64,128]{2,1,0:T(8,128)(2,1)} %stack.119), calls=%async_computation.2 | async-start | bytes 131072 | tf_op jit(solution)/shard_map/all_to_all | solution.py:33
  41.3 8.2 %all_gather.20 = bf16[512,128]{1,0:T(8,128)(2,1)S(1)} all-gather(bf16[64,128]{1,0:T(8,128)(2,1)S(1)} %get-tuple-element.24), channel_id=1, replica_groups=mesh['row'=8,'col'=4] {'row'}, dimensions={0}, use_global_device_ids=true | all-gather | bytes 147456 | tf_op jit(solution)/shard_map/all_gather | solution.py:10
  49.5 0.0 all-to-all-done.2
  49.5 0.2 fusion.32
  49.7 0.6 stack.120
  50.3 5.1 %all-to-all-start.3 = ((bf16[4,64,128]{2,1,0:T(8,128)(2,1)}), bf16[4,64,128]{2,1,0:T(8,128)(2,1)S(1)}, u32[]{:S(2)}, u32[]{:S(2)}) async-start(bf16[4,64,128]{2,1,0:T(8,128)(2,1)} %stack.120), calls=%async_computation.3 | async-start | bytes 131072 | tf_op jit(solution)/shard_map/all_to_all | solution.py:33
  57.3 9.2 %all_gather.21 = bf16[512,128]{1,0:T(8,128)(2,1)S(1)} all-gather(bf16[64,128]{1,0:T(8,128)(2,1)S(1)} %get-tuple-element.22), channel_id=1, replica_groups=mesh['row'=8,'col'=4] {'row'}, dimensions={0}, use_global_device_ids=true | all-gather | bytes 147456 | tf_op jit(solution)/shard_map/all_gather | solution.py:10
  66.5 0.0 all-to-all-done.3
  66.5 0.2 fusion.31
  66.7 0.6 stack.121
  67.3 5.1 %all-to-all-start.4 = ((bf16[4,64,128]{2,1,0:T(8,128)(2,1)}), bf16[4,64,128]{2,1,0:T(8,128)(2,1)S(1)}, u32[]{:S(2)}, u32[]{:S(2)}) async-start(bf16[4,64,128]{2,1,0:T(8,128)(2,1)} %stack.121), calls=%async_computation.4 | async-start | bytes 131072 | tf_op jit(solution)/shard_map/all_to_all | solution.py:33
  72.4 8.2 %all_gather.22 = bf16[512,128]{1,0:T(8,128)(2,1)S(1)} all-gather(bf16[64,128]{1,0:T(8,128)(2,1)S(1)} %get-tuple-element.20), channel_id=1, replica_groups=mesh['row'=8,'col'=4] {'row'}, dimensions={0}, use_global_device_ids=true | all-gather | bytes 147456 | tf_op jit(solution)/shard_map/all_gather | solution.py:10
  80.6 0.0 all-to-all-done.4
  80.6 0.2 fusion.30
  80.8 0.6 stack.122
  81.4 5.1 %all-to-all-start.5 = ((bf16[4,64,128]{2,1,0:T(8,128)(2,1)}), bf16[4,64,128]{2,1,0:T(8,128)(2,1)S(1)}, u32[]{:S(2)}, u32[]{:S(2)}) async-start(bf16[4,64,128]{2,1,0:T(8,128)(2,1)} %stack.122), calls=%async_computation.5 | async-start | bytes 131072 | tf_op jit(solution)/shard_map/all_to_all | solution.py:33
  86.5 9.2 %all_gather.23 = bf16[512,128]{1,0:T(8,128)(2,1)S(1)} all-gather(bf16[64,128]{1,0:T(8,128)(2,1)S(1)} %get-tuple-element.18), channel_id=1, replica_groups=mesh['row'=8,'col'=4] {'row'}, dimensions={0}, use_global_device_ids=true | all-gather | bytes 147456 | tf_op jit(solution)/shard_map/all_gather | solution.py:10
  95.7 0.0 all-to-all-done.5
  95.7 1.5 %fusion.28 = (f32[]{:T(128)}, f32[]{:T(128)}, f32[]{:T(128)}, f32[]{:T(128)}, f32[]{:T(128)}, /*index=5*/f32[]{:T(128)}, f32[]{:T(128)}, f32[]{:T(128)}, f32[]{:...) fusion(f32[64,128]{1,0:T(8,128)S(1)} %get-tuple-element.19, s32[128]{0:T(128)S(1)} %iota_add_fusion, ...), kind=kOutput, calls=%fused_computation.46 | convolution fusion | flops 8617972 | bytes 590641 | tf_op jit(solution)/shard_map/dot_general | solution.py:37
  97.2 1.4 maximum_bitcast_fusion.5
  98.6 0.1 copy.17
  98.7 1.3 maximum_bitcast_fusion.4
  99.9 0.1 copy.16
  100.0 1.3 maximum_bitcast_fusion.3
  101.4 0.1 copy.15
  101.5 1.3 maximum_bitcast_fusion.2
  102.8 0.1 copy.14
  102.9 1.3 maximum_bitcast_fusion.1
  104.2 0.1 copy.13
  104.3 1.3 maximum_bitcast_fusion
  105.6 0.1 copy.12
  105.7 0.1 stack.147
  105.8 39.8 %psum.7 = f32[6,2]{0,1:T(2,128)S(1)} all-reduce(f32[6,2]{0,1:T(2,128)S(1)} %stack.147), channel_id=1, replica_groups=mesh['row'=8,'col'=4] {'row','col'}, use_global_device_ids=true, to_apply=%region_12.13 | all-reduce | flops 12 | bytes 96 | tf_op jit(solution)/shard_map/psum | solution.py:47
  145.6 0.6 broadcast_multiply_fusion
  (2 shorter events, 0.0 us)
Async XLA Ops:
  2.0 6.5 %copy-start.1 = (s32[6]{0:T(128)S(1)}, s32[6]{0:T(128)}, u32[]{:S(2)}) copy-start(s32[6]{0:T(128)} %param.3) | copy-start | bytes 76
  2.0 17.1 %all-to-all-start = ((bf16[4,64,128]{2,1,0:T(8,128)(2,1)}), bf16[4,64,128]{2,1,0:T(8,128)(2,1)S(1)}, u32[]{:S(2)}, u32[]{:S(2)}) async-start(bf16[4,64,128]{2,1,0:T(8,128)(2,1)} %stack.117), calls=%async_computation | async-start | bytes 131072 | tf_op jit(solution)/shard_map/all_to_all | solution.py:33
  9.9 9.2 %copy-start = (f32[64,128]{1,0:T(8,128)S(1)}, f32[64,128]{1,0:T(8,128)}, u32[]{:S(2)}) copy-start(f32[64,128]{1,0:T(8,128)} %param.2) | copy-start | bytes 98308
  19.9 14.8 %all-to-all-start.1 = ((bf16[4,64,128]{2,1,0:T(8,128)(2,1)}), bf16[4,64,128]{2,1,0:T(8,128)(2,1)S(1)}, u32[]{:S(2)}, u32[]{:S(2)}) async-start(bf16[4,64,128]{2,1,0:T(8,128)(2,1)} %stack.118), calls=%async_computation.1 | async-start | bytes 131072 | tf_op jit(solution)/shard_map/all_to_all | solution.py:33
  35.6 14.0 %all-to-all-start.2 = ((bf16[4,64,128]{2,1,0:T(8,128)(2,1)}), bf16[4,64,128]{2,1,0:T(8,128)(2,1)S(1)}, u32[]{:S(2)}, u32[]{:S(2)}) async-start(bf16[4,64,128]{2,1,0:T(8,128)(2,1)} %stack.119), calls=%async_computation.2 | async-start | bytes 131072 | tf_op jit(solution)/shard_map/all_to_all | solution.py:33
  50.3 16.2 %all-to-all-start.3 = ((bf16[4,64,128]{2,1,0:T(8,128)(2,1)}), bf16[4,64,128]{2,1,0:T(8,128)(2,1)S(1)}, u32[]{:S(2)}, u32[]{:S(2)}) async-start(bf16[4,64,128]{2,1,0:T(8,128)(2,1)} %stack.120), calls=%async_computation.3 | async-start | bytes 131072 | tf_op jit(solution)/shard_map/all_to_all | solution.py:33
  67.3 13.3 %all-to-all-start.4 = ((bf16[4,64,128]{2,1,0:T(8,128)(2,1)}), bf16[4,64,128]{2,1,0:T(8,128)(2,1)S(1)}, u32[]{:S(2)}, u32[]{:S(2)}) async-start(bf16[4,64,128]{2,1,0:T(8,128)(2,1)} %stack.121), calls=%async_computation.4 | async-start | bytes 131072 | tf_op jit(solution)/shard_map/all_to_all | solution.py:33
  81.4 14.3 %all-to-all-start.5 = ((bf16[4,64,128]{2,1,0:T(8,128)(2,1)}), bf16[4,64,128]{2,1,0:T(8,128)(2,1)S(1)}, u32[]{:S(2)}, u32[]{:S(2)}) async-start(bf16[4,64,128]{2,1,0:T(8,128)(2,1)} %stack.122), calls=%async_computation.5 | async-start | bytes 131072 | tf_op jit(solution)/shard_map/all_to_all | solution.py:33
